TPU v7x, 32 devices: a whole 2x2x4 slice. The times are simulated.
32 devices in a mesh: groups: 2 (over x), space: 16 (over z, y, core).
Axes of the slice: x: 2, y: 2, z: 4, core: 2. Of those that a mesh axis runs over, the one named last changes fastest.
Arguments:
- inputs: bfloat16 [768, 1152, 256], P(('groups', 'space')), parts along dimension 0, may hold values from -6 to 6
- spectral_weight: bfloat16 [2, 256, 2, 256, 256], P(None, 'space'), may hold values from -0.25 to 0.25
- local_weight: bfloat16 [2, 256, 256], replicated, may hold values from -0.375 to 0.375
- layer_bias: bfloat16 [2, 256], replicated, may hold values from -3 to 3
- readout_hidden: bfloat16 [256, 256], replicated, may hold values from -0.375 to 0.375
- readout_final: bfloat16 [20, 256], replicated, may hold values from -0.375 to 0.375
Outputs:
- forecast: bfloat16 [20, 768, 1152], P(None, ('groups', 'space')), parts along dimension 1
There are 2 independent parts, one for each index of `groups`. A program takes and returns all parts, laid end to end along the dimension named above; an argument that names none is the same for every part. Nothing has to cross between parts.
All inputs are finite; a program needn't handle non-finite values.
Results may differ from a plain program's by a relative error of at most 0.018.
Values may be sent and summed in bfloat16 or wider, within the bound.
A program may use at most 128 MiB of HBM per device.

v0:
```python
import jax
import jax.numpy as jnp
from jax import lax
from jax.sharding import PartitionSpec as P

KY = 16
KX = 16
LAYERS = 2
MODES = 256


def zonal_tables(columns, modes):
    column_ids = jnp.arange(columns, dtype=jnp.int32)
    wave_numbers = jnp.arange(1, modes + 1, dtype=jnp.int32)
    phase_int = column_ids[:, None] * wave_numbers[None, :] % columns
    angles = 2.0 * jnp.pi / columns * phase_int.astype(jnp.float32)
    cosines = jnp.cos(angles)
    sines = jnp.sin(angles)
    forward = jnp.concatenate([cosines, -sines], axis=1) / jnp.sqrt(jnp.float32(columns))
    inverse = jnp.stack([cosines, -sines], axis=2).reshape(columns, 2 * modes) * jnp.sqrt(
        jnp.float32(2.0 / modes)
    )
    return (forward.astype(jnp.bfloat16), inverse.astype(jnp.bfloat16))


def meridional_tables(row_ids, height, modes):
    mode_index = jnp.arange(modes, dtype=jnp.int32)
    wave_numbers = jnp.where(mode_index < modes // 2, mode_index, mode_index - modes)
    phase_int = wave_numbers[:, None] * row_ids[None, :] % height
    angles = 2.0 * jnp.pi / height * phase_int.astype(jnp.float32)
    cosines = jnp.cos(angles)
    sines = jnp.sin(angles)
    forward = jnp.stack(
        [jnp.stack([cosines, sines], axis=2), jnp.stack([-sines, cosines], axis=2)], axis=1
    )
    forward = forward / jnp.sqrt(jnp.float32(height))
    cos_rows = cosines.T
    sin_rows = sines.T
    inverse = jnp.stack(
        [jnp.stack([cos_rows, -sin_rows], axis=2), jnp.stack([sin_rows, cos_rows], axis=2)], axis=1
    )
    inverse = inverse / jnp.sqrt(jnp.float32(modes))
    return (forward.astype(jnp.bfloat16), inverse.astype(jnp.bfloat16))


def mix_modes(spectrum, weights):
    real_in = spectrum[:, 0]
    imag_in = spectrum[:, 1]
    real_weight = weights[:, 0]
    imag_weight = weights[:, 1]

    def product(vectors, matrices):
        return jnp.einsum("mi,mio->mo", vectors, matrices, preferred_element_type=jnp.float32)

    real_out = product(real_in, real_weight) - product(imag_in, imag_weight)
    imag_out = product(real_in, imag_weight) + product(imag_in, real_weight)
    return jnp.stack([real_out, imag_out], axis=1).astype(jnp.bfloat16)


def per_device(inputs, spectral_weight, local_weight, layer_bias, readout_hidden, readout_final):
    rows_here, columns, channels = inputs.shape
    devices_along = lax.axis_size("space")
    height = rows_here * devices_along
    zonal_forward, zonal_inverse = zonal_tables(columns, KX)
    local_rows = jnp.arange(rows_here, dtype=jnp.int32) * devices_along + lax.axis_index("space")
    forward_here, inverse_here = meridional_tables(local_rows, height, KY)
    current = inputs
    for layer_index in range(LAYERS):
        zonal_part = jnp.einsum(
            "hwc,wj->hjc", current, zonal_forward, preferred_element_type=jnp.float32
        )
        zonal_view = zonal_part.astype(jnp.bfloat16).reshape(rows_here, 2, KX, channels)
        partial_value = jnp.einsum(
            "qphr,hrkc->qkpc", forward_here, zonal_view, preferred_element_type=jnp.float32
        )
        partial_value = partial_value.reshape(MODES, 2 * channels)
        spectrum = lax.psum_scatter(
            partial_value, "space", scatter_dimension=0, tiled=True
        ).reshape(-1, 2, channels)
        mixed = mix_modes(spectrum.astype(jnp.bfloat16), spectral_weight[layer_index])
        all_modes = lax.all_gather(mixed, "space", axis=0, tiled=True).reshape(KY, KX, 2, channels)
        returned = jnp.einsum(
            "hpqr,qkrc->hkpc", inverse_here, all_modes, preferred_element_type=jnp.float32
        )
        returned = returned.astype(jnp.bfloat16).reshape(rows_here, 2 * KX, channels)
        spread = jnp.einsum(
            "wj,hjc->hwc", zonal_inverse, returned, preferred_element_type=jnp.float32
        )
        pointwise = jnp.dot(
            current.reshape(-1, channels),
            local_weight[layer_index],
            preferred_element_type=jnp.float32,
        )
        pointwise = pointwise.reshape(current.shape)
        bias_now = layer_bias[layer_index].astype(jnp.float32)
        current = jax.nn.gelu(spread + pointwise + bias_now, approximate=True).astype(jnp.bfloat16)
    hidden = jnp.dot(
        current.reshape(-1, channels), readout_hidden, preferred_element_type=jnp.float32
    )
    hidden = jax.nn.gelu(hidden, approximate=True).astype(jnp.bfloat16)
    final = jnp.einsum("pq,nq->pn", readout_final, hidden, preferred_element_type=jnp.float32)
    return final.astype(jnp.bfloat16).reshape(readout_final.shape[0], rows_here, columns)


def solution(mesh):
    in_specs = (
        P(("groups", "space"), None, None),
        P(None, "space", None, None, None),
        P(),
        P(),
        P(),
        P(),
    )
    out_specs = P(None, ("groups", "space"), None)
    return jax.shard_map(
        per_device, mesh=mesh, in_specs=in_specs, out_specs=out_specs, check_vma=False
    )
```

profile of v0, /device:TPU:0, one launch (start us, length us, event | category | flops | bytes accessed | tf_op | source)
XLA Modules:
  0.0 308.6 jit_solution(3359486465415475526)
XLA Ops:
  6.5 0.0 copy-start
  6.5 0.0 copy-start.1
  6.5 0.0 reduce-scatter.3.cloned.1.call-start
  6.6 0.4 fusion.64
  7.0 0.1 fusion.101
  7.1 7.5 %convolution_convert_fusion.2 = bf16[32,24,256]{2,0,1:T(8,128)(2,1)S(1)} fusion(bf16[24,1152,256]{2,1,0:T(8,128)(2,1)} %param.6, f32[1152,16]{0,1:T(8,128)S(1)} %get-tuple-element.26, f32[1152,16]{0,1:T(8,128)S(1)} %get-tuple-element.25), kind=kOutput, calls=%fused_computation.49 | convolution fusion | flops 453292032 | bytes 14696448 | tf_op jit(solution)/shard_map/hwc,wj->hjc/dot_general | solution.py:69
  14.6 0.4 convolution_bitcast_fusion.3
  15.0 0.4 copy.42
  15.4 0.8 copy.96
  16.3 0.0 reduce-scatter.3.cloned.1.call-update
  16.3 0.0 reduce-scatter.5.cloned.1.call-start
  16.3 0.1 fusion.110
  16.5 0.4 fusion.61
  16.9 0.0 copy-done.1
  16.9 6.0 %slice_bitcast_fusion.1 = (bf16[16,2,256,256]{3,2,1,0:T(8,128)(2,1)}, bf16[16,2,256,256]{3,2,1,0:T(8,128)(2,1)}) fusion(bf16[2,16,2,256,256]{4,3,2,1,0:T(8,128)(2,1)} %param.7), kind=kLoop, calls=%fused_computation.33 | loop fusion | bytes 16777216 | tf_op jit(solution)/shard_map/squeeze | solution.py:80
  22.8 52.5 %reduce-scatter.3.cloned.1.call-done = f32[16,512]{1,0:T(8,128)} async-done(((f32[256,512]{1,0:T(8,128)}), f32[16,512]{1,0:T(8,128)}) %reduce-scatter.3.cloned.1.call-update) | async-done | bytes 32784 | tf_op jit(solution)/shard_map/reduce_scatter | solution.py:77
  75.3 0.8 convert_element_type.150
  76.1 2.0 fusion.29
  78.1 2.0 fusion.28
  80.1 2.0 fusion.27
  82.1 2.0 fusion.30
  84.1 20.3 %all_gather.6 = bf16[256,2,256]{2,0,1:T(8,128)(2,1)S(1)} all-gather(bf16[16,2,256]{2,0,1:T(8,128)(2,1)S(1)} %pad_maximum_fusion), channel_id=1, replica_groups=mesh['groups'=2,'space'=16] {'space'}, dimensions={0}, use_global_device_ids=true | all-gather | bytes 278528 | tf_op jit(solution)/shard_map/all_gather | solution.py:81
  104.4 0.3 fusion.38
  104.7 0.0 copy-start.2
  104.7 11.4 %fusion.43 = f32[24,256,1152,1]{2,1,3,0:T(8,128)} fusion(bf16[24,16,2,256]{3,0,2,1:T(8,128)(2,1)S(1)} %fusion.38, f32[1152,16,1]{0,1,2:T(8,128)S(1)} %get-tuple-element.24, f32[1152,16,1]{0,1,2:T(8,128)S(1)} %get-tuple-element.23), kind=kOutput, calls=%fused_computation.60 | convolution fusion | flops 453095424 | bytes 28852224 | tf_op jit(solution)/shard_map/wj,hjc->hwc/dot_general | solution.py:86
  116.1 0.0 copy-done.2
  116.1 24.0 %fusion.7 = bf16[24,1152,256]{1,2,0:T(8,128)(2,1)} fusion(f32[24,256,1152,1]{2,1,3,0:T(8,128)} %fusion.43, bf16[24,1152,256]{2,1,0:T(8,128)(2,1)} %param.6, f32[256]{0:T(256)S(1)} %bitcast.212, bf16[2,256,256]{2,1,0:T(8,128)(2,1)S(1)} %copy-done.2), kind=kOutput, calls=%fused_computation.11 | convolution fusion | flops 3701735424 | bytes 56755200 | tf_op jit(solution)/shard_map/dot_general | solution.py:89
  140.1 9.3 %convolution_convert_fusion.1 = bf16[32,24,256]{2,0,1:T(8,128)(2,1)S(1)} fusion(bf16[24,1152,256]{1,2,0:T(8,128)(2,1)} %fusion.7, f32[1152,16]{0,1:T(8,128)S(1)} %get-tuple-element.26, f32[1152,16]{0,1:T(8,128)S(1)} %get-tuple-element.25), kind=kOutput, calls=%fused_computation.48 | convolution fusion | flops 453292032 | bytes 14696448 | tf_op jit(solution)/shard_map/hwc,wj->hjc/dot_general | solution.py:69
  149.4 0.3 convolution_bitcast_fusion.2
  149.8 0.4 copy.50
  150.2 0.8 copy.97
  151.0 0.0 reduce-scatter.5.cloned.1.call-update
  151.0 53.6 %reduce-scatter.5.cloned.1.call-done = f32[16,512]{1,0:T(8,128)} async-done(((f32[256,512]{1,0:T(8,128)}), f32[16,512]{1,0:T(8,128)}) %reduce-scatter.5.cloned.1.call-update) | async-done | bytes 32784 | tf_op jit(solution)/shard_map/reduce_scatter | solution.py:77
  204.6 0.8 convert_element_type.163
  205.4 2.0 fusion.31
  207.4 2.0 fusion.34
  209.4 2.0 fusion.33
  211.3 2.0 fusion.32
  213.4 20.3 %all_gather.7 = bf16[256,2,256]{2,0,1:T(8,128)(2,1)S(1)} all-gather(bf16[16,2,256]{2,0,1:T(8,128)(2,1)S(1)} %pad_maximum_fusion.1), channel_id=1, replica_groups=mesh['groups'=2,'space'=16] {'space'}, dimensions={0}, use_global_device_ids=true | all-gather | bytes 278528 | tf_op jit(solution)/shard_map/all_gather | solution.py:81
  233.7 0.3 fusion.37
  234.0 11.4 %fusion.41 = f32[24,256,1152,1]{2,1,3,0:T(8,128)} fusion(bf16[24,16,2,256]{3,0,2,1:T(8,128)(2,1)S(1)} %fusion.37, f32[1152,16,1]{0,1,2:T(8,128)S(1)} %get-tuple-element.24, f32[1152,16,1]{0,1,2:T(8,128)S(1)} %get-tuple-element.23), kind=kOutput, calls=%fused_computation.58 | convolution fusion | flops 453095424 | bytes 28852224 | tf_op jit(solution)/shard_map/wj,hjc->hwc/dot_general | solution.py:86
  245.4 24.4 %fusion.15 = bf16[24,1152,256]{1,2,0:T(8,128)(2,1)} fusion(f32[24,256,1152,1]{2,1,3,0:T(8,128)} %fusion.41, bf16[24,1152,256]{1,2,0:T(8,128)(2,1)} %fusion.7, f32[256]{0:T(256)S(1)} %bitcast.211, bf16[2,256,256]{2,1,0:T(8,128)(2,1)S(1)} %copy-done.2), kind=kOutput, calls=%fused_computation.19 | convolution fusion | flops 3701735424 | bytes 56755200 | tf_op jit(solution)/shard_map/dot_general | solution.py:89
  269.8 18.7 %copy.57 = bf16[24,1152,256]{2,1,0:T(8,128)(2,1)} copy(bf16[24,1152,256]{1,2,0:T(8,128)(2,1)} %fusion.15) | data formatting | bytes 28311552 | tf_op jit(solution)/shard_map/convert_element_type | solution.py:96
  288.5 0.0 copy-done
  288.5 0.0 copy-done.3
  288.5 12.0 %convolution_convert_fusion = bf16[27648,20]{0,1:T(8,128)(2,1)S(1)} fusion(bf16[20,256]{1,0:T(8,128)(2,1)S(1)} %copy-done.3, bf16[27648,256]{1,0:T(8,128)(2,1)} %bitcast.196, bf16[256,256]{1,0:T(8,128)(2,1)S(1)} %copy-done), kind=kOutput, calls=%fused_computation.3 | convolution fusion | flops 3971248128 | bytes 15403008 | tf_op jit(solution)/shard_map/pq,nq->pn/dot_general | solution.py:101
  300.5 0.2 copy.98
  300.6 1.1 slice.64
  (20 shorter events, 0.2 us)
Async XLA Ops:
  6.5 282.0 %copy-start = (bf16[256,256]{1,0:T(8,128)(2,1)S(1)}, bf16[256,256]{1,0:T(8,128)(2,1)}, u32[]{:S(2)}) copy-start(bf16[256,256]{1,0:T(8,128)(2,1)} %param.10) | copy-start | bytes 393220
  6.5 10.3 %copy-start.1 = (bf16[2,256]{1,0:T(2,128)(2,1)S(1)}, bf16[2,256]{1,0:T(2,128)(2,1)}, u32[]{:S(2)}) copy-start(bf16[2,256]{1,0:T(2,128)(2,1)} %param.9) | copy-start | bytes 3076
  6.5 68.8 %reduce-scatter.3.cloned.1.call-start = ((), (), s32[]{:S(2)}) async-start(), calls=%async_computation.2 | async-start | bytes 557056 | tf_op jit(solution)/shard_map/reduce_scatter | solution.py:77
  16.3 188.3 %reduce-scatter.5.cloned.1.call-start = ((), (), s32[]{:S(2)}) async-start(), calls=%async_computation.3 | async-start | bytes 557056 | tf_op jit(solution)/shard_map/reduce_scatter | solution.py:77
  104.7 11.4 %copy-start.2 = (bf16[2,256,256]{2,1,0:T(8,128)(2,1)S(1)}, bf16[2,256,256]{2,1,0:T(8,128)(2,1)}, u32[]{:S(2)}) copy-start(bf16[2,256,256]{2,1,0:T(8,128)(2,1)} %param.8) | copy-start | bytes 786436
  269.8 18.7 %copy-start.3 = (bf16[20,256]{1,0:T(8,128)(2,1)S(1)}, bf16[20,256]{1,0:T(8,128)(2,1)}, u32[]{:S(2)}) copy-start(bf16[20,256]{1,0:T(8,128)(2,1)} %param.11) | copy-start | bytes 30724
Sparse Core Ops, SparseCore 0:
  16.4 58.8 reduce-scatter.2
  151.1 53.3 reduce-scatter.4
where the time goes:
time: 310 us; the launch traced here: 309 us
  matrix products  117 us (38%)
  waiting for transfers between devices  106 us (34%)
  blocking collectives  40.7 us (13%)
  local copies, waits for them, and re-layouts  28.5 us (9%)
  between operations  13.6 us (4%)
    reduce_scatter x2, waiting for transfers between devices, per_device(): lax.psum_scatter(partial_value, 'space', scatter_dimension=0, tiled=True)  106 us
    dot_general x2, matrix products, per_device(): jnp.dot(current.reshape(-1, channels), local_weight[layer_index], preferr...  48.4 us
    all_gather x2, blocking collectives, per_device(): lax.all_gather(mixed, 'space', axis=0, tiled=True)  40.7 us
    dot_general x2, matrix products, per_device(): jnp.einsum('wj,hjc->hwc', zonal_inverse, returned, preferred_element_type...  22.8 us
    convert_element_type x1, local copies, waits for them, and re-layouts, per_device(): jax.nn.gelu(spread + pointwise + bias_now, approximate=True)  18.7 us
    dot_general x2, matrix products, per_device(): jnp.einsum('hwc,wj->hjc', current, zonal_forward, preferred_element_type=...  16.8 us
    dot_general x8, matrix products, product(): jnp.einsum('mi,mio->mo', vectors, matrices, preferred_element_type=jnp.fl...  15.8 us
    dot_general x1, matrix products, per_device(): jnp.einsum('pq,nq->pn', readout_final, hidden, preferred_element_type=jnp...  12 us
  transfers between devices with their start and end apart: 2, of which 2 were waited for; matrix products, arithmetic and copies ran while one was open for 2% of the time, Pallas kernels for 0%

commit v1 on v0

v1 whole, which is shorter than its diff:
```python
import functools

import jax
import jax.numpy as jnp
import numpy as np
from jax import lax
from jax.experimental import pallas as pl
from jax.experimental.pallas import tpu as pltpu
from jax.sharding import PartitionSpec as P

KY = 16
KX = 16
LAYERS = 2
MODES = KY * KX
BF16 = jnp.bfloat16
F32 = jnp.float32
VMEM_LIMIT = 60 * 1024 * 1024


def zonal_tables(columns):
    phase = np.arange(columns)[:, None] * np.arange(1, KX + 1)[None, :] % columns
    angles = np.float32(2.0 * np.pi / columns) * phase.astype(np.float32)
    cosines, sines = np.cos(angles), np.sin(angles)
    forward = np.concatenate([cosines, -sines], axis=1) / np.sqrt(np.float32(columns))
    inverse = np.stack([cosines, -sines], axis=2).reshape(columns, 2 * KX)
    inverse = inverse * np.sqrt(np.float32(2.0 / KX))
    extended = np.zeros((columns, 128), np.float32)
    extended[:, : 2 * KX] = inverse
    extended[:, 2 * KX] = 1.0
    return forward.T.astype(BF16), extended.astype(BF16)


def meridional_tables(rows_here, devices):
    height = rows_here * devices
    rows = np.arange(rows_here)[None, :] * devices + np.arange(devices)[:, None]
    index = np.arange(KY)
    waves = np.where(index < KY // 2, index, index - KY)
    phase = waves[None, :, None] * rows[:, None, :] % height
    angles = np.float32(2.0 * np.pi / height) * phase.astype(np.float32)
    cosines, sines = np.cos(angles), np.sin(angles)
    forward = np.stack(
        [np.stack([cosines, sines], -1), np.stack([-sines, cosines], -1)], axis=2
    ) / np.sqrt(np.float32(height))
    cos_rows, sin_rows = cosines.transpose(0, 2, 1), sines.transpose(0, 2, 1)
    inverse = np.stack(
        [np.stack([cos_rows, -sin_rows], -1), np.stack([sin_rows, cos_rows], -1)], axis=2
    ) / np.sqrt(np.float32(KY))
    return (
        forward.reshape(devices, 2 * KY, 2 * rows_here).astype(BF16),
        inverse.reshape(devices, 2 * rows_here, 2 * KY).astype(BF16),
    )


def one_hot(values, count):
    return (values[:, None] == np.arange(count)[None, :]).astype(BF16)


def expanded_tables(rows_here, devices, me):
    forward, inverse = meridional_tables(rows_here, devices)
    owned = MODES // devices
    spectral = np.arange(2 * MODES)
    mode = spectral // (2 * owned) * owned + spectral % owned
    part = spectral // owned % 2
    spectral_wave = mode % KX
    spectral_qp = mode // KX * 2 + part
    rows = np.arange(rows_here * 2 * KX)
    zonal_hr, zonal_wave = rows // KX, rows % KX
    back_hp, back_wave = rows // (2 * KX) * 2 + rows % 2, rows % (2 * KX) // 2
    here = lax.dynamic_index_in_dim(jnp.asarray(forward), me, keepdims=False)
    back = lax.dynamic_index_in_dim(jnp.asarray(inverse), me, keepdims=False)
    pick_qp = jnp.asarray(one_hot(spectral_qp, 2 * KY))

    def spread_out(left, middle, right, left_wave, right_wave):
        inner = jnp.dot(left, middle, preferred_element_type=F32).astype(BF16)
        full = jnp.dot(inner, right, preferred_element_type=F32)
        same = jnp.asarray(left_wave, jnp.int32)[:, None] == jnp.asarray(right_wave, jnp.int32)[None, :]
        return jnp.where(same, full, 0.0).astype(BF16)

    ahead = spread_out(
        pick_qp, here, jnp.asarray(one_hot(zonal_hr, 2 * rows_here).T), spectral_wave, zonal_wave
    )
    behind = spread_out(
        jnp.asarray(one_hot(back_hp, 2 * rows_here)), back, pick_qp.T, back_wave, spectral_wave
    )
    return ahead, behind


def gelu(v):
    inner = v * (0.7978845608028654 + (0.7978845608028654 * 0.044715) * (v * v))
    half = 0.5 * v
    return half + half * jnp.tanh(inner)


def analyse_row(zonal_ref, held_ref, state, row):
    part = jnp.dot(zonal_ref[...], state, preferred_element_type=F32)
    depth = zonal_ref.shape[0]
    held_ref[pl.ds(pl.multiple_of(row * depth, depth), depth), :] = part.astype(BF16)


def analyse_end(ahead_ref, held_ref, partial_ref):
    @pl.when(pl.program_id(0) == pl.num_programs(0) - 1)
    def _():
        sums = jnp.dot(ahead_ref[...], held_ref[...], preferred_element_type=F32)
        partial_ref[...] = sums.reshape(partial_ref.shape).astype(partial_ref.dtype)


def first_kernel(state_ref, zonal_ref, ahead_ref, partial_ref, held_ref):
    rows = state_ref.shape[0]
    for r in range(rows):
        analyse_row(zonal_ref, held_ref, state_ref[r], pl.program_id(0) * rows + r)
    analyse_end(ahead_ref, held_ref, partial_ref)


def update(state_ref, r, start, size, spread_ref, weight_ref, back_ref, bias_ref):
    left = jnp.concatenate(
        [state_ref[r, pl.ds(start, size), :], spread_ref[pl.ds(start, size), :]], axis=1
    )
    depth = 2 * KX
    back = back_ref[pl.ds(r * depth, depth), :]
    right = jnp.concatenate([weight_ref[...], back, bias_ref[...]], axis=0)
    return gelu(jnp.dot(left, right, preferred_element_type=F32)).astype(BF16)


def middle_kernel(
    chunk, state_ref, back_ref, spread_ref, weight_ref, bias_ref, zonal_ref, ahead_ref,
    next_ref, partial_ref, held_ref,
):
    rows, columns = state_ref.shape[:2]
    for r in range(rows):
        for start in range(0, columns, chunk):
            next_ref[r, pl.ds(start, chunk), :] = update(
                state_ref, r, start, chunk, spread_ref, weight_ref, back_ref, bias_ref
            )
        analyse_row(zonal_ref, held_ref, next_ref[r], pl.program_id(0) * rows + r)
    analyse_end(ahead_ref, held_ref, partial_ref)


def last_kernel(
    chunk, rows_here, state_ref, back_ref, spread_ref, weight_ref, bias_ref, hidden_ref, final_ref,
    out_ref, held_ref,
):
    rows, columns = state_ref.shape[:2]
    count = final_ref.shape[0]
    for r in range(rows):
        row = pl.program_id(0) * rows + r
        for start in range(0, columns, chunk):
            state = update(
                state_ref, r, start, chunk, spread_ref, weight_ref, back_ref, bias_ref
            )
            hidden = gelu(
                jnp.dot(state, hidden_ref[...], preferred_element_type=F32)
            ).astype(BF16)
            final = lax.dot_general(
                final_ref[...], hidden, (((1,), (1,)), ((), ())), preferred_element_type=F32
            )
            for lane in range(0, chunk, 128):
                held_ref[
                    (start + lane) // 128, pl.ds(row, count, stride=rows_here), :
                ] = final[:, lane : lane + 128]

    @pl.when(pl.program_id(0) == pl.num_programs(0) - 1)
    def _():
        for block in range(columns // 128):
            out_ref[:, pl.ds(block * 128, 128)] = held_ref[block].astype(BF16)


def exchange_kernel(
    layer, n, partial_ref, weight_hbm, behind_ref, back_ref,
    weights, arrived, mixed_ref, gathered, weight_sem, sent, received, sent_mixed, received_mixed,
):
    me = lax.axis_index("space")
    load = pltpu.make_async_copy(weight_hbm.at[layer], weights, weight_sem)
    load.start()
    barrier = pltpu.get_barrier_semaphore()
    for i in range(1, n):
        pl.semaphore_signal(barrier, inc=1, device_id={"space": lax.rem(me + i, n)})
    pl.semaphore_wait(barrier, n - 1)

    def part_copy(i):
        to = lax.rem(me + i, n)
        return pltpu.make_async_remote_copy(
            src_ref=partial_ref.at[to], dst_ref=arrived.at[i], send_sem=sent.at[i],
            recv_sem=received.at[i], device_id={"space": to},
        )

    def mixed_copy(i):
        return pltpu.make_async_remote_copy(
            src_ref=mixed_ref, dst_ref=gathered.at[me], send_sem=sent_mixed.at[i],
            recv_sem=received_mixed.at[i], device_id={"space": lax.rem(me + i, n)},
        )

    for i in range(1, n):
        part_copy(i).start()
    total = partial_ref[me].astype(F32)
    for i in range(1, n):
        part_copy(i).wait_recv()
        total = total + arrived[i].astype(F32)
    spectrum = total.astype(BF16)
    load.wait()
    owned = total.shape[0] // 2
    row = lax.broadcasted_iota(jnp.int32, (owned, total.shape[1]), 0)
    real = jnp.zeros((owned, total.shape[1]), F32)
    imag = jnp.zeros((owned, total.shape[1]), F32)
    for m in range(owned):
        by_real = jnp.dot(spectrum, weights[m, 0], preferred_element_type=F32)
        by_imag = jnp.dot(spectrum, weights[m, 1], preferred_element_type=F32)
        real = jnp.where(row == m, by_real[:owned] - by_imag[owned:], real)
        imag = jnp.where(row == m, by_imag[:owned] + by_real[owned:], imag)
    mixed = jnp.concatenate([real, imag], axis=0).astype(BF16)
    mixed_ref[...] = mixed
    for i in range(1, n):
        mixed_copy(i).start()
    gathered[me] = mixed
    for i in range(1, n):
        mixed_copy(i).wait_recv()
    modes = gathered[...].astype(F32).reshape(n * 2 * owned, -1).astype(BF16)
    back_ref[...] = jnp.dot(behind_ref[...], modes, preferred_element_type=F32).astype(BF16)
    for i in range(1, n):
        part_copy(i).wait_send()
        mixed_copy(i).wait_send()


def whole(shape):
    return pl.BlockSpec(shape, lambda i: (0,) * len(shape))


def params():
    return pltpu.CompilerParams(
        dimension_semantics=("arbitrary",), vmem_limit_bytes=VMEM_LIMIT
    )


def pick_chunk(columns):
    for chunk in (384, 256, 128):
        if columns % chunk == 0:
            return chunk
    return columns


def per_device(inputs, spectral_weight, local_weight, layer_bias, readout_hidden, readout_final):
    rows_here, columns, channels = inputs.shape
    n = lax.axis_size("space")
    owned = MODES // n
    depth = 2 * KX
    step = 2 if rows_here % 2 == 0 else 1
    steps = rows_here // step
    chunk = pick_chunk(columns)
    count = readout_final.shape[0]
    zonal_np, spread_np = zonal_tables(columns)
    zonal, spread = jnp.asarray(zonal_np), jnp.asarray(spread_np)
    ahead, behind = expanded_tables(rows_here, n, lax.axis_index("space"))
    bias_rows = jnp.pad(layer_bias[:, None, :], ((0, 0), (0, 127 - depth), (0, 0)))

    state_spec = pl.BlockSpec((step, columns, channels), lambda i: (i, 0, 0))
    back_spec = pl.BlockSpec((step * depth, channels), lambda i: (i, 0))
    partial_shape = (n, 2 * owned, channels)
    partial_out = jax.ShapeDtypeStruct(partial_shape, BF16)
    held = pltpu.VMEM((rows_here * depth, channels), BF16)

    def exchange(layer, partial):
        vmem = pl.BlockSpec(memory_space=pltpu.VMEM)
        return pl.pallas_call(
            functools.partial(exchange_kernel, layer, n),
            name=f"exchange_{layer}",
            out_shape=jax.ShapeDtypeStruct((rows_here * depth, channels), BF16),
            in_specs=[vmem, pl.BlockSpec(memory_space=pl.ANY), vmem],
            out_specs=vmem,
            scratch_shapes=[
                pltpu.VMEM((owned, 2, channels, channels), BF16),
                pltpu.VMEM(partial_shape, BF16),
                pltpu.VMEM((2 * owned, channels), BF16),
                pltpu.VMEM(partial_shape, BF16),
                pltpu.SemaphoreType.DMA,
                pltpu.SemaphoreType.DMA((n,)),
                pltpu.SemaphoreType.DMA((n,)),
                pltpu.SemaphoreType.DMA((n,)),
                pltpu.SemaphoreType.DMA((n,)),
            ],
            compiler_params=pltpu.CompilerParams(
                collective_id=layer, has_side_effects=True, vmem_limit_bytes=VMEM_LIMIT
            ),
        )(partial, spectral_weight, behind)

    partial = pl.pallas_call(
        first_kernel,
        name="first",
        grid=(steps,),
        out_shape=partial_out,
        in_specs=[state_spec, whole(zonal.shape), whole(ahead.shape)],
        out_specs=whole(partial_shape),
        scratch_shapes=[held],
        compiler_params=params(),
    )(inputs, zonal, ahead)
    current = inputs
    for layer in range(LAYERS - 1):
        back = exchange(layer, partial)
        current, partial = pl.pallas_call(
            functools.partial(middle_kernel, chunk),
            name=f"middle_{layer}",
            grid=(steps,),
            out_shape=(jax.ShapeDtypeStruct(inputs.shape, BF16), partial_out),
            in_specs=[
                state_spec, back_spec, whole(spread.shape), whole((channels, channels)),
                whole(bias_rows.shape[1:]), whole(zonal.shape), whole(ahead.shape),
            ],
            out_specs=(state_spec, whole(partial_shape)),
            scratch_shapes=[held],
            compiler_params=params(),
        )(current, back, spread, local_weight[layer], bias_rows[layer], zonal, ahead)
    layer = LAYERS - 1
    back = exchange(layer, partial)
    forecast = pl.pallas_call(
        functools.partial(last_kernel, chunk, rows_here),
        name="last",
        grid=(steps,),
        out_shape=jax.ShapeDtypeStruct((count * rows_here, columns), BF16),
        in_specs=[
            state_spec, back_spec, whole(spread.shape), whole((channels, channels)),
            whole(bias_rows.shape[1:]), whole(readout_hidden.shape), whole(readout_final.shape),
        ],
        out_specs=whole((count * rows_here, columns)),
        scratch_shapes=[pltpu.VMEM((columns // 128, count * rows_here, 128), F32)],
        compiler_params=params(),
    )(current, back, spread, local_weight[layer], bias_rows[layer], readout_hidden, readout_final)
    return forecast.reshape(count, rows_here, columns)


def solution(mesh):
    in_specs = (
        P(("groups", "space"), None, None),
        P(None, "space", None, None, None),
        P(),
        P(),
        P(),
        P(),
    )
    out_specs = P(None, ("groups", "space"), None)
    return jax.shard_map(
        per_device, mesh=mesh, in_specs=in_specs, out_specs=out_specs, check_vma=False
    )
```

time: 310 us -> 125 us (0.40)
  Pallas kernels: 0 us -> 117 us
  matrix products: 117 us -> 4.65 us
  waiting for transfers between devices: 106 us -> 0 us
  blocking collectives: 40.7 us -> 0 us
  local copies, waits for them, and re-layouts: 28.5 us -> 3.05 us
  between operations: 13.6 us -> 0.04 us
    pallas_call x0 -> x5, Pallas kernels: none -> 117 us  [the longest x2 43 us: exchange(): pl.pallas_call(functools.partial(exchange_kernel, layer, n), name=f'excha...]
    dot_general x19 -> x2, matrix products: 117 us -> 4.65 us  [spread_out(): full = jnp.dot(inner, right, preferred_element_type=F32)]
    reduce_scatter x2 -> x0, waiting for transfers between devices: 106 us -> none  [per_device(): lax.psum_scatter(partial_value, 'space', scatter_dimension=0, tiled=True)]
    all_gather x2 -> x0, blocking collectives: 40.7 us -> none  [per_device(): lax.all_gather(mixed, 'space', axis=0, tiled=True)]
    convert_element_type x3 -> x0, local copies, waits for them, and re-layouts: 18.7 us -> none  [the longest x1 18.7 us: per_device(): jax.nn.gelu(spread + pointwise + bias_now, approximate=True)]
    squeeze x2, local copies, waits for them, and re-layouts: 5.96 us -> 2.35 us  [the longest x1 1.7 us: per_device(): local_weight[layer]]
  transfers between devices with their start and end apart: 2 -> 0, of which waited for: 2 -> 0; matrix products, arithmetic and copies ran while one was open for 2% -> 0% of each run, Pallas kernels for 0% -> 0%
where the time goes in v1:
time: 125 us
  Pallas kernels  117 us (94%)
  matrix products  4.65 us (4%)
  local copies, waits for them, and re-layouts  3.05 us (2%)
    pallas_call x2, Pallas kernels, exchange(): pl.pallas_call(functools.partial(exchange_kernel, layer, n), name=f'excha...  43 us
    pallas_call x1, Pallas kernels, per_device(): pl.pallas_call(functools.partial(last_kernel, chunk, rows_here), name='la...  40.6 us
    pallas_call x1, Pallas kernels, per_device(): pl.pallas_call(functools.partial(middle_kernel, chunk), name=f'middle_{la...  21.6 us
    pallas_call x1, Pallas kernels, per_device(): pl.pallas_call(first_kernel, name='first', grid=(steps,), out_shape=parti...  11.7 us
    dot_general x2, matrix products, spread_out(): full = jnp.dot(inner, right, preferred_element_type=F32)  4.65 us

profile of v1, /device:TPU:0, one launch (start us, length us, event | category | flops | bytes accessed | tf_op | source)
XLA Modules:
  0.0 124.6 jit_solution(10417594495155497168)
XLA Ops:
  0.0 0.7 copy.18
  0.7 0.7 fusion.1
  1.3 1.7 %slice_bitcast_fusion = (bf16[256,256]{1,0:T(8,128)(2,1)}, bf16[256,256]{1,0:T(8,128)(2,1)}) fusion(bf16[2,256,256]{2,1,0:T(8,128)(2,1)} %param.19), kind=kLoop, calls=%fused_computation.6 | loop fusion | bytes 524288 | tf_op jit(solution)/shard_map/squeeze | solution.py:324
  3.0 2.4 %select_convert_fusion.1.ahead_ref = bf16[512,768]{1,0:T(8,128)(2,1)} fusion(bf16[48,768]{1,0:T(8,128)(2,1)} %constant.44.clone, bf16[512,32]{1,0:T(8,128)(2,1)} %constant.43.clone, s32[768]{0:T(1024)} %constant.46.clone, s32[512]{0:T(512)} %constant.45.clone, bf16[16,32,48]{2,1,0:T(8,128)(2,1)} %constant.41.clone, s32[]{:T(128)S(6)} %select_n.14), kind=kOutput, calls=%fused_computation.1 | convolution fusion | flops 40525824 | bytes 1005572 | tf_op jit(solution)/shard_map/dot_general | solution.py:75
  5.5 0.0 copy-start
  5.5 0.0 copy-start.1
  5.5 0.0 copy-start.2
  5.5 0.0 copy-start.3
  5.5 11.7 %first.1.partial_ref = bf16[16,32,256]{2,1,0:T(8,128)(2,1)} custom-call(bf16[24,1152,256]{2,1,0:T(8,128)(2,1)} %state_ref.3, bf16[32,1152]{1,0:T(8,128)(2,1)} %constant.39.clone.zonal_ref, bf16[512,768]{1,0:T(8,128)(2,1)} %select_convert_fusion.1.ahead_ref), custom_call_target="tpu_custom_call" | custom-call | tf_op jit(solution)/shard_map/first/pallas_call | solution.py:284
  17.2 0.0 copy-done
  17.2 0.0 copy-done.1
  17.2 0.0 copy-done.2
  17.2 0.0 copy-done.3
  17.2 2.2 %select_convert_fusion.behind_ref = bf16[768,512]{1,0:T(8,128)(2,1)} fusion(bf16[512,32]{1,0:T(8,128)(2,1)S(1)} %copy-done.1, bf16[768,48]{1,0:T(8,128)(2,1)S(1)} %copy-done, s32[512]{0:T(512)S(1)} %copy-done.3, s32[768]{0:T(1024)S(1)} %copy-done.2, bf16[16,48,32]{2,1,0:T(8,128)(2,1)} %constant.42.clone, s32[]{:T(128)S(6)} %select_n.14), kind=kOutput, calls=%fused_computation | convolution fusion | flops 28729344 | bytes 910340 | tf_op jit(solution)/shard_map/dot_general | solution.py:75
  19.4 22.1 %exchange_0.1.back_ref = bf16[768,256]{1,0:T(8,128)(2,1)} custom-call(bf16[16,32,256]{2,1,0:T(8,128)(2,1)} %first.1.partial_ref, bf16[2,16,2,256,256]{4,3,2,1,0:T(8,128)(2,1)} %weight_hbm.3, bf16[768,512]{1,0:T(8,128)(2,1)} %select_convert_fusion.behind_ref), custom_call_target="tpu_custom_call" | custom-call | tf_op jit(solution)/shard_map/exchange_0/pallas_call | solution.py:262
  41.5 21.6 %middle_0.1 = (bf16[24,1152,256]{2,1,0:T(8,128)(2,1)}, bf16[16,32,256]{2,1,0:T(8,128)(2,1)}) custom-call(bf16[24,1152,256]{2,1,0:T(8,128)(2,1)} %state_ref.3, bf16[768,256]{1,0:T(8,128)(2,1)} %exchange_0.1.back_ref, bf16[1152,128]{1,0:T(8,128)(2,1)} %constant.40.clone.spread_ref, bf16[256,256]{1,0:T(8,128)(2,1)} %get-tuple-element.10.weight_ref, ...), custom_call_target="tpu_custom_call" | custom-call | tf_op jit(solution)/shard_map/middle_0/pallas_call | solution.py:297
  63.1 20.9 %exchange_1.1.back_ref = bf16[768,256]{1,0:T(8,128)(2,1)} custom-call(bf16[16,32,256]{2,1,0:T(8,128)(2,1)} %get-tuple-element.8.partial_ref, bf16[2,16,2,256,256]{4,3,2,1,0:T(8,128)(2,1)} %weight_hbm.3, bf16[768,512]{1,0:T(8,128)(2,1)} %select_convert_fusion.behind_ref), custom_call_target="tpu_custom_call" | custom-call | tf_op jit(solution)/shard_map/exchange_1/pallas_call | solution.py:262
  84.0 40.6 %last.1 = bf16[480,1152]{1,0:T(8,128)(2,1)} custom-call(bf16[24,1152,256]{2,1,0:T(8,128)(2,1)} %get-tuple-element.7.state_ref, bf16[768,256]{1,0:T(8,128)(2,1)} %exchange_1.1.back_ref, bf16[1152,128]{1,0:T(8,128)(2,1)} %constant.40.clone.spread_ref, bf16[256,256]{1,0:T(8,128)(2,1)} %get-tuple-element.9.weight_ref, ...), custom_call_target="tpu_custom_call" | custom-call | tf_op jit(solution)/shard_map/last/pallas_call | solution.py:312
Async XLA Ops:
  5.5 11.7 %copy-start = (bf16[768,48]{1,0:T(8,128)(2,1)S(1)}, bf16[768,48]{1,0:T(8,128)(2,1)}, u32[]{:S(2)}) copy-start(bf16[768,48]{1,0:T(8,128)(2,1)} %constant.47.clone) | copy-start | bytes 221188
  5.5 11.7 %copy-start.1 = (bf16[512,32]{1,0:T(8,128)(2,1)S(1)}, bf16[512,32]{1,0:T(8,128)(2,1)}, u32[]{:S(2)}) copy-start(bf16[512,32]{1,0:T(8,128)(2,1)} %constant.43.clone) | copy-start | bytes 98308
  5.5 11.7 %copy-start.2 = (s32[768]{0:T(1024)S(1)}, s32[768]{0:T(1024)}, u32[]{:S(2)}) copy-start(s32[768]{0:T(1024)} %constant.48.clone) | copy-start | bytes 9220
  5.5 11.7 %copy-start.3 = (s32[512]{0:T(512)S(1)}, s32[512]{0:T(512)}, u32[]{:S(2)}) copy-start(s32[512]{0:T(512)} %constant.45.clone) | copy-start | bytes 6148

commit v2 on v0

v2 whole, which is shorter than its diff:
```python
import functools

import jax
import jax.numpy as jnp
import numpy as np
from jax import lax
from jax.experimental import pallas as pl
from jax.experimental.pallas import tpu as pltpu
from jax.sharding import PartitionSpec as P

KY = 16
KX = 16
LAYERS = 2
MODES = KY * KX
BF16 = jnp.bfloat16
F32 = jnp.float32
VMEM_LIMIT = 62 * 1024 * 1024
GELU_TYPE = BF16
SLOPE = 0.7978845608028654


def zonal_tables(columns):
    phase = np.arange(columns)[:, None] * np.arange(1, KX + 1)[None, :] % columns
    angles = np.float32(2.0 * np.pi / columns) * phase.astype(np.float32)
    cosines, sines = np.cos(angles), np.sin(angles)
    forward = np.concatenate([cosines, -sines], axis=1) / np.sqrt(np.float32(columns))
    inverse = np.stack([cosines, -sines], axis=2).reshape(columns, 2 * KX)
    inverse = inverse * np.sqrt(np.float32(2.0 / KX))
    extended = np.zeros((columns, 128), np.float32)
    extended[:, : 2 * KX] = inverse
    extended[:, 2 * KX] = 1.0
    return forward.T.astype(BF16), extended.astype(BF16)


def meridional_tables(rows_here, devices):
    height = rows_here * devices
    rows = np.arange(rows_here)[None, :] * devices + np.arange(devices)[:, None]
    index = np.arange(KY)
    waves = np.where(index < KY // 2, index, index - KY)
    phase = waves[None, :, None] * rows[:, None, :] % height
    angles = np.float32(2.0 * np.pi / height) * phase.astype(np.float32)
    cosines, sines = np.cos(angles), np.sin(angles)
    forward = np.stack(
        [np.stack([cosines, sines], -1), np.stack([-sines, cosines], -1)], axis=2
    ) / np.sqrt(np.float32(height))
    cos_rows, sin_rows = cosines.transpose(0, 2, 1), sines.transpose(0, 2, 1)
    inverse = np.stack(
        [np.stack([cos_rows, -sin_rows], -1), np.stack([sin_rows, cos_rows], -1)], axis=2
    ) / np.sqrt(np.float32(KY))
    return (
        forward.reshape(devices, 2 * KY, 2 * rows_here).astype(BF16),
        inverse.reshape(devices, 2 * rows_here, 2 * KY).astype(BF16),
    )


def shift_of(value):
    shift = value.bit_length() - 1
    assert 1 << shift == value
    return shift


def expand_tables(owned, forward, inverse, ahead_ref, behind_ref):
    wave_bits, owned_bits = shift_of(KX), shift_of(owned)

    def split(shape, axis):
        index = lax.broadcasted_iota(jnp.int32, shape, axis)
        part = (index >> owned_bits) & 1
        mode = ((index >> (owned_bits + 1)) << owned_bits) + (index & (owned - 1))
        return mode & (KX - 1), (mode >> wave_bits) * 2 + part

    def iota(shape, axis):
        return lax.broadcasted_iota(jnp.int32, shape, axis)

    def ones(mask):
        return jnp.where(mask, 1.0, 0.0).astype(BF16)

    def product(left, middle, right, same):
        inner = jnp.dot(left, middle, preferred_element_type=F32).astype(BF16)
        full = jnp.dot(inner, right, preferred_element_type=F32)
        return jnp.where(same, full, 0.0).astype(BF16)

    modes, wide = ahead_ref.shape
    narrow = forward.shape[1]
    qp = forward.shape[0]
    pick = ones(split((modes, qp), 0)[1] == iota((modes, qp), 1))
    rows = ones(iota((narrow, wide), 0) == iota((narrow, wide), 1) >> wave_bits)
    same = split((modes, wide), 0)[0] == iota((modes, wide), 1) & (KX - 1)
    ahead_ref[...] = product(pick, forward, rows, same)
    index = iota((wide, narrow), 0)
    rows = ones((index >> (wave_bits + 1)) * 2 + (index & 1) == iota((wide, narrow), 1))
    pick = ones(split((qp, modes), 1)[1] == iota((qp, modes), 0))
    same = (iota((wide, modes), 0) & (2 * KX - 1)) >> 1 == split((wide, modes), 1)[0]
    behind_ref[...] = product(rows, inverse, pick, same)


def gelu_of_half(half):
    half = half.astype(GELU_TYPE)
    inner = half * (SLOPE * 2.0 + (SLOPE * 0.044715 * 8.0) * (half * half))
    return (half + half * jnp.tanh(inner)).astype(BF16)


def program_kernel(
    n, chunk, state_hbm, weight_hbm, local_ref, bias_ref, hidden_ref, final_ref,
    zonal_ref, spread_ref, forward_ref, inverse_ref, out_ref,
    state_a, state_b, weights, ahead, behind, right, hidden_half, held, back,
    partial, arrived, mixed_ref, gathered, finals,
    state_sem, weight_sem, sent, received, sent_mixed, received_mixed,
):
    me = lax.axis_index("space")
    rows_here, columns, channels = state_a.shape
    owned = weights.shape[1]
    depth = 2 * KX
    count = final_ref.shape[0]
    load_rows = 2 if rows_here % 2 == 0 else 1
    work_rows = next(k for k in (4, 3, 2, 1) if rows_here % k == 0)
    last_rows = load_rows

    def state_copy(j):
        rows = pl.ds(j * load_rows, load_rows)
        return pltpu.make_async_copy(state_hbm.at[rows], state_a.at[rows], state_sem.at[j])

    def weight_copy(layer):
        return pltpu.make_async_copy(
            weight_hbm.at[layer], weights.at[layer], weight_sem.at[layer]
        )

    def part_copy(layer, i):
        to = lax.rem(me + i, n)
        return pltpu.make_async_remote_copy(
            src_ref=partial.at[layer, to], dst_ref=arrived.at[layer, i],
            send_sem=sent.at[layer, i], recv_sem=received.at[layer, i],
            device_id={"space": to},
        )

    def mixed_copy(layer, i):
        return pltpu.make_async_remote_copy(
            src_ref=mixed_ref.at[layer], dst_ref=gathered.at[layer, me],
            send_sem=sent_mixed.at[layer, i], recv_sem=received_mixed.at[layer, i],
            device_id={"space": lax.rem(me + i, n)},
        )

    for j in range(rows_here // load_rows):
        state_copy(j).start()
    for layer in range(LAYERS):
        weight_copy(layer).start()
    barrier = pltpu.get_barrier_semaphore()
    for i in range(1, n):
        pl.semaphore_signal(barrier, inc=1, device_id={"space": lax.rem(me + i, n)})
    expand_tables(owned, forward_ref[me], inverse_ref[me], ahead, behind)
    hidden_half[...] = (0.5 * hidden_ref[...].astype(F32)).astype(BF16)

    def analyse(state, row):
        part = jnp.dot(zonal_ref[...], state[row], preferred_element_type=F32)
        held[pl.ds(pl.multiple_of(row * depth, depth), depth), :] = part.astype(BF16)

    def exchange(layer):
        sums = jnp.dot(ahead[...], held[...], preferred_element_type=F32)
        partial[layer] = sums.reshape(n, 2 * owned, channels).astype(BF16)
        if layer == 0:
            pl.semaphore_wait(barrier, n - 1)
        for i in range(1, n):
            part_copy(layer, i).start()
        total = partial[layer, me].astype(F32)
        first = lax.broadcasted_iota(jnp.int32, (128 - depth, channels), 0) == 0
        bias = bias_ref[layer : layer + 1, :].astype(F32)
        right[:channels, :] = (0.5 * local_ref[layer].astype(F32)).astype(BF16)
        right[channels:, :] = jnp.where(first, 0.5 * bias, 0.0).astype(BF16)
        weight_copy(layer).wait()
        for i in range(1, n):
            part_copy(layer, i).wait_recv()
            total = total + arrived[layer, i].astype(F32)
        spectrum = total.astype(BF16)
        row = lax.broadcasted_iota(jnp.int32, (owned, channels), 0)
        real = jnp.zeros((owned, channels), F32)
        imag = jnp.zeros((owned, channels), F32)
        for m in range(owned):
            by_real = jnp.dot(spectrum, weights[layer, m, 0], preferred_element_type=F32)
            by_imag = jnp.dot(spectrum, weights[layer, m, 1], preferred_element_type=F32)
            real = jnp.where(row == m, by_real[:owned] - by_imag[owned:], real)
            imag = jnp.where(row == m, by_imag[:owned] + by_real[owned:], imag)
        mixed = jnp.concatenate([real, imag], axis=0).astype(BF16)
        mixed_ref[layer] = mixed
        for i in range(1, n):
            mixed_copy(layer, i).start()
        gathered[layer, me] = mixed
        for i in range(1, n):
            mixed_copy(layer, i).wait_recv()
        modes = gathered[layer].astype(F32).reshape(n * 2 * owned, channels).astype(BF16)
        values = jnp.dot(behind[...], modes, preferred_element_type=F32).astype(BF16)
        back[...] = (0.5 * values.astype(F32)).astype(BF16)
        for i in range(1, n):
            part_copy(layer, i).wait_send()
            mixed_copy(layer, i).wait_send()

    def update(state, row, start):
        columns_now = pl.ds(start, chunk)
        left = jnp.concatenate([state[row, columns_now, :], spread_ref[columns_now, :]], axis=1)
        returned = back[pl.ds(pl.multiple_of(row * depth, depth), depth), :]
        table = jnp.concatenate([right[:channels, :], returned, right[channels:, :]], axis=0)
        return gelu_of_half(jnp.dot(left, table, preferred_element_type=F32))

    def first_step(j, carry):
        state_copy(j).wait()
        for r in range(load_rows):
            analyse(state_a, j * load_rows + r)
        return carry

    lax.fori_loop(0, rows_here // load_rows, first_step, 0)
    source, target = state_a, state_b
    for layer in range(LAYERS - 1):
        exchange(layer)

        def middle_step(j, carry, source=source, target=target):
            for r in range(work_rows):
                row = j * work_rows + r
                for start in range(0, columns, chunk):
                    target[row, pl.ds(start, chunk), :] = update(source, row, start)
                analyse(target, row)
            return carry

        lax.fori_loop(0, rows_here // work_rows, middle_step, 0)
        source, target = target, source
    exchange(LAYERS - 1)

    def last_step(j, carry):
        for r in range(last_rows):
            row = j * last_rows + r
            for start in range(0, columns, chunk):
                state = update(source, row, start)
                hidden = gelu_of_half(
                    jnp.dot(state, hidden_half[...], preferred_element_type=F32)
                )
                final = lax.dot_general(
                    final_ref[...], hidden, (((1,), (1,)), ((), ())), preferred_element_type=F32
                )
                for lane in range(0, chunk, 128):
                    finals[
                        (start + lane) // 128, pl.ds(row, count, stride=rows_here), :
                    ] = final[:, lane : lane + 128]
        return carry

    lax.fori_loop(0, rows_here // last_rows, last_step, 0)
    for block in range(columns // 128):
        out_ref[:, pl.ds(block * 128, 128)] = finals[block].astype(BF16)


def pick_chunk(columns):
    return next((chunk for chunk in (384, 256, 128) if columns % chunk == 0), columns)


def per_device(inputs, spectral_weight, local_weight, layer_bias, readout_hidden, readout_final):
    rows_here, columns, channels = inputs.shape
    n = lax.axis_size("space")
    owned = MODES // n
    depth = 2 * KX
    count = readout_final.shape[0]
    zonal, spread = zonal_tables(columns)
    forward, inverse = meridional_tables(rows_here, n)
    vmem = pl.BlockSpec(memory_space=pltpu.VMEM)
    anywhere = pl.BlockSpec(memory_space=pl.ANY)
    chunks = (LAYERS, n, 2 * owned, channels)
    dma = pltpu.SemaphoreType.DMA
    forecast = pl.pallas_call(
        functools.partial(program_kernel, n, pick_chunk(columns)),
        name="program",
        out_shape=jax.ShapeDtypeStruct((count * rows_here, columns), BF16),
        in_specs=[anywhere, anywhere] + [vmem] * 8,
        out_specs=vmem,
        scratch_shapes=[
            pltpu.VMEM(inputs.shape, BF16),
            pltpu.VMEM(inputs.shape, BF16),
            pltpu.VMEM((LAYERS, owned, 2, channels, channels), BF16),
            pltpu.VMEM((2 * MODES, rows_here * depth), BF16),
            pltpu.VMEM((rows_here * depth, 2 * MODES), BF16),
            pltpu.VMEM((channels + 128 - depth, channels), BF16),
            pltpu.VMEM(readout_hidden.shape, BF16),
            pltpu.VMEM((rows_here * depth, channels), BF16),
            pltpu.VMEM((rows_here * depth, channels), BF16),
            pltpu.VMEM(chunks, BF16),
            pltpu.VMEM(chunks, BF16),
            pltpu.VMEM((LAYERS, 2 * owned, channels), BF16),
            pltpu.VMEM(chunks, BF16),
            pltpu.VMEM((columns // 128, count * rows_here, 128), F32),
            dma((rows_here,)),
            dma((LAYERS,)),
            dma((LAYERS, n)),
            dma((LAYERS, n)),
            dma((LAYERS, n)),
            dma((LAYERS, n)),
        ],
        compiler_params=pltpu.CompilerParams(
            collective_id=0, has_side_effects=True, vmem_limit_bytes=VMEM_LIMIT
        ),
    )(
        inputs, spectral_weight, local_weight, layer_bias, readout_hidden, readout_final,
        jnp.asarray(zonal), jnp.asarray(spread), jnp.asarray(forward), jnp.asarray(inverse),
    )
    return forecast.reshape(count, rows_here, columns)


def solution(mesh):
    in_specs = (
        P(("groups", "space"), None, None),
        P(None, "space", None, None, None),
        P(),
        P(),
        P(),
        P(),
    )
    out_specs = P(None, ("groups", "space"), None)
    return jax.shard_map(
        per_device, mesh=mesh, in_specs=in_specs, out_specs=out_specs, check_vma=False
    )
```

time: 310 us -> 99.6 us (0.32)
  matrix products: 117 us -> 0 us
  waiting for transfers between devices: 106 us -> 0 us
  Pallas kernels: 0 us -> 96.5 us
  blocking collectives: 40.7 us -> 0 us
  local copies, waits for them, and re-layouts: 28.5 us -> 2.32 us
  between operations: 13.6 us -> 0.01 us
    dot_general x19 -> x0, matrix products: 117 us -> none  [the longest x2 48.4 us: per_device(): jnp.dot(current.reshape(-1, channels), local_weight[layer_index], preferr...]
    reduce_scatter x2 -> x0, waiting for transfers between devices: 106 us -> none  [per_device(): lax.psum_scatter(partial_value, 'space', scatter_dimension=0, tiled=True)]
    pallas_call x0 -> x1, Pallas kernels: none -> 96.5 us  [per_device(): pl.pallas_call(functools.partial(program_kernel, n, pick_chunk(columns)),...]
    all_gather x2 -> x0, blocking collectives: 40.7 us -> none  [per_device(): lax.all_gather(mixed, 'space', axis=0, tiled=True)]
    convert_element_type x3 -> x0, local copies, waits for them, and re-layouts: 18.7 us -> none  [the longest x1 18.7 us: per_device(): jax.nn.gelu(spread + pointwise + bias_now, approximate=True)]
    squeeze x2 -> x0, local copies, waits for them, and re-layouts: 5.96 us -> none  [the longest x1 5.95 us: per_device(): spectral_weight[layer_index]]
  transfers between devices with their start and end apart: 2 -> 0, of which waited for: 2 -> 0; matrix products, arithmetic and copies ran while one was open for 2% -> 0% of each run, Pallas kernels for 0% -> 0%
where the time goes in v2:
time: 99.6 us; the launch traced here: 98.9 us
  Pallas kernels  96.5 us (97%)
  local copies, waits for them, and re-layouts  2.32 us (2%)
    pallas_call x1, Pallas kernels, per_device(): pl.pallas_call(functools.partial(program_kernel, n, pick_chunk(columns)),...  96.5 us
    unnamed x1, local copies, waits for them, and re-layouts  2.32 us

profile of v2, /device:TPU:0, one launch (start us, length us, event | category | flops | bytes accessed | tf_op | source)
XLA Modules:
  0.0 98.9 jit_solution(16545876513556561672)
XLA Ops:
  0.0 96.5 %program.1 = bf16[480,1152]{1,0:T(8,128)(2,1)} custom-call(bf16[24,1152,256]{2,1,0:T(8,128)(2,1)} %state_hbm.1, bf16[2,16,2,256,256]{4,3,2,1,0:T(8,128)(2,1)} %weight_hbm.1, bf16[2,256,256]{2,1,0:T(8,128)(2,1)} %local_ref.1, bf16[2,256]{1,0:T(2,128)(2,1)} %bias_ref.1, bf16[256,256]{1,0:T(8,128)(2,1)} %hidden_ref.1, bf16[20,256]{1,0:T(8,128)(2,1)} %final_ref.1, ...), custom_call_target="tpu_custom_call" | custom-call | tf_op jit(solution)/shard_map/program/pallas_call | solution.py:263
  96.5 2.3 %copy.12 = bf16[20,24,1152]{2,1,0:T(8,128)(2,1)} copy(bf16[20,24,1152]{2,1,0:T(8,128)(2,1)} %bitcast.1) | data formatting | bytes 2211840
